TPU v7x, 32 devices: a whole 2x2x4 slice. The times are simulated.
32 devices in a mesh: dp: 2 (over x), tp: 4 (over z), sp: 4 (over y, core).
Axes of the slice: x: 2, y: 2, z: 4, core: 2. Of those that a mesh axis runs over, the one named last changes fastest.
Arguments:
- embeds: bfloat16 [16384, 2304], P(('dp', 'sp')), parts along dimension 0
- positions: int32 [16384], P(('dp', 'sp')), parts along dimension 0
- w_query: bfloat16 [2, 2304, 8, 256], P(None, None, 'tp')
- w_key: bfloat16 [2, 2304, 4, 256], P(None, None, 'tp')
- w_value: bfloat16 [2, 2304, 4, 256], P(None, None, 'tp')
- w_out: bfloat16 [2, 8, 256, 2304], P(None, 'tp')
- w_gate: bfloat16 [2, 2304, 9216], P(None, None, 'tp')
- w_up: bfloat16 [2, 2304, 9216], P(None, None, 'tp')
- w_down: bfloat16 [2, 9216, 2304], P(None, 'tp')
- attn_gain: bfloat16 [2, 2304], replicated
- mlp_gain: bfloat16 [2, 2304], replicated
Outputs:
- output 1: bfloat16 [16384, 2304], P(('dp', 'sp')), parts along dimension 0
- output 2: bfloat16 [2, 16384, 4, 256], P(None, ('dp', 'sp'), 'tp'), parts along dimension 1
- output 3: bfloat16 [2, 16384, 4, 256], P(None, ('dp', 'sp'), 'tp'), parts along dimension 1
There are 2 independent parts. A program takes and returns all parts, laid end to end along the dimension named above; an argument that names none is the same for every part.
All inputs are finite; a program needn't handle non-finite values.
Results may differ from a plain program's by a relative error of at most 0.02.
Values are sent between devices in bfloat16 or wider.
A program may use at most 1 GiB of HBM per device.

v0:
```python
import jax
import jax.numpy as jnp
from jax import lax
from jax.sharding import PartitionSpec as P

ROPE_BASE = 10000.0
NORM_EPS = 1e-6
WINDOW = 1024
QUERY_ROWS = 512


def rms_norm(hidden, gain_vec):
    hidden_f = hidden.astype(jnp.float32)
    inv_rms = lax.rsqrt(jnp.mean(hidden_f * hidden_f, axis=-1, keepdims=True) + NORM_EPS)
    return (hidden_f * inv_rms * gain_vec.astype(jnp.float32)).astype(jnp.bfloat16)


def rotary(head_vals, positions):
    head_dim = head_vals.shape[-1]
    half_dim = head_dim // 2
    inv_freq = ROPE_BASE ** (-2.0 * jnp.arange(half_dim, dtype=jnp.float32) / head_dim)
    angles = positions.astype(jnp.float32)[:, None] * inv_freq[None, :]
    cosine = jnp.cos(angles)[:, None, :]
    sine_val = jnp.sin(angles)[:, None, :]
    heads_f = head_vals.astype(jnp.float32)
    first_half = heads_f[..., :half_dim]
    second_half = heads_f[..., half_dim:]
    rotated = jnp.concatenate([first_half * cosine - second_half * sine_val, second_half * cosine + first_half * sine_val], axis=-1)
    return rotated.astype(jnp.bfloat16)


def softmax_rows(logits, visible):
    masked = jnp.where(visible, logits, -1e30)
    row_peak = jnp.max(masked, axis=-1, keepdims=True)
    weights = jnp.exp(masked - row_peak)
    return (weights / jnp.sum(weights, axis=-1, keepdims=True)).astype(jnp.bfloat16)


def attend_rows(q_rows, k_rows, v_rows, q_index, k_index, window):
    qk_scale = q_rows.shape[-1] ** -0.5
    logits = jnp.einsum('tkgd,skd->tkgs', q_rows, k_rows, preferred_element_type=jnp.float32) * qk_scale
    dist_rows = q_index[:, None] - k_index[None, :]
    visible = (dist_rows >= 0) & (k_index[None, :] >= 0)
    if window:
        visible = visible & (dist_rows <= window)
    probs_bf = softmax_rows(logits, visible[:, None, None, :])
    return jnp.einsum('tkgs,skd->tkgd', probs_bf, v_rows, preferred_element_type=jnp.float32).astype(jnp.bfloat16)


def full_attention(queries, keys_all, values_all, q_start):
    num_rows = min(QUERY_ROWS, queries.shape[0])
    k_index = jnp.arange(keys_all.shape[0])

    def one_block(block_id):
        row_start = block_id * num_rows
        q_rows = lax.dynamic_slice_in_dim(queries, row_start, num_rows, 0)
        q_index = q_start + row_start + jnp.arange(num_rows)
        return attend_rows(q_rows, keys_all, values_all, q_index, k_index, 0)

    blocks_out = lax.map(one_block, jnp.arange(queries.shape[0] // num_rows))
    return blocks_out.reshape(queries.shape)


def window_attention(queries, keys_ext, values_ext, q_start):
    num_rows = min(QUERY_ROWS, queries.shape[0])
    key_span = WINDOW + num_rows

    def one_block(block_id):
        row_start = block_id * num_rows
        q_rows = lax.dynamic_slice_in_dim(queries, row_start, num_rows, 0)
        k_rows = lax.dynamic_slice_in_dim(keys_ext, row_start, key_span, 0)
        v_rows = lax.dynamic_slice_in_dim(values_ext, row_start, key_span, 0)
        q_index = q_start + row_start + jnp.arange(num_rows)
        k_index = q_start + row_start - WINDOW + jnp.arange(key_span)
        return attend_rows(q_rows, k_rows, v_rows, q_index, k_index, WINDOW)

    blocks_out = lax.map(one_block, jnp.arange(queries.shape[0] // num_rows))
    return blocks_out.reshape(queries.shape)


def solution(mesh):
    seq_count = mesh.shape['sp']
    shift_pairs = [(src_idx, src_idx + 1) for src_idx in range(seq_count - 1)]
    row_spec = P(('dp', 'sp'), None)
    pos_spec = P(('dp', 'sp'))
    head_cols = P(None, None, 'tp', None)
    head_rows = P(None, 'tp', None, None)
    ff_cols = P(None, None, 'tp')
    ff_rows = P(None, 'tp', None)
    gain_spec = P(None, None)
    cache_spec = P(None, ('dp', 'sp'), 'tp', None)

    def device_step(embeds, positions, w_query, w_key, w_value, w_out, w_gate, w_up, w_down, attn_gain, mlp_gain):
        num_tokens = embeds.shape[0]
        q_start = lax.axis_index('sp') * num_tokens
        kv_local = w_key.shape[2]
        head_dim = w_key.shape[3]
        group_size = w_query.shape[2] // kv_local
        hidden = embeds
        k_layers = []
        v_layers = []
        for layer_id in range(w_query.shape[0]):
            normed = rms_norm(hidden, attn_gain[layer_id])
            queries = jnp.einsum('td,dhe->the', normed, w_query[layer_id], preferred_element_type=jnp.float32).astype(jnp.bfloat16)
            keys_loc = jnp.einsum('td,dhe->the', normed, w_key[layer_id], preferred_element_type=jnp.float32).astype(jnp.bfloat16)
            values_loc = jnp.einsum('td,dhe->the', normed, w_value[layer_id], preferred_element_type=jnp.float32).astype(jnp.bfloat16)
            queries = rotary(queries, positions).reshape(num_tokens, kv_local, group_size, head_dim)
            keys_loc = rotary(keys_loc, positions)
            if layer_id % 2 == 0:
                halo_k = lax.ppermute(keys_loc[num_tokens - WINDOW:], 'sp', shift_pairs)
                halo_v = lax.ppermute(values_loc[num_tokens - WINDOW:], 'sp', shift_pairs)
                keys_ext = jnp.concatenate([halo_k, keys_loc], axis=0)
                values_ext = jnp.concatenate([halo_v, values_loc], axis=0)
                attn_rows = window_attention(queries, keys_ext, values_ext, q_start)
            else:
                keys_all = lax.all_gather(keys_loc, 'sp', axis=0, tiled=True)
                values_all = lax.all_gather(values_loc, 'sp', axis=0, tiled=True)
                attn_rows = full_attention(queries, keys_all, values_all, q_start)
            attn_part = jnp.einsum('thd,hde->te', attn_rows.reshape(num_tokens, kv_local * group_size, head_dim), w_out[layer_id], preferred_element_type=jnp.float32)
            attn_sum = lax.psum(attn_part, 'tp').astype(jnp.bfloat16)
            hidden = (hidden.astype(jnp.float32) + attn_sum.astype(jnp.float32)).astype(jnp.bfloat16)
            normed = rms_norm(hidden, mlp_gain[layer_id])
            gate_proj = jnp.dot(normed, w_gate[layer_id], preferred_element_type=jnp.float32)
            up_proj = jnp.dot(normed, w_up[layer_id], preferred_element_type=jnp.float32)
            hidden_act = (jax.nn.silu(gate_proj) * up_proj).astype(jnp.bfloat16)
            mlp_part = jnp.dot(hidden_act, w_down[layer_id], preferred_element_type=jnp.float32)
            mlp_sum = lax.psum(mlp_part, 'tp').astype(jnp.bfloat16)
            hidden = (hidden.astype(jnp.float32) + mlp_sum.astype(jnp.float32)).astype(jnp.bfloat16)
            k_layers.append(keys_loc)
            v_layers.append(values_loc)
        return hidden, jnp.stack(k_layers), jnp.stack(v_layers)

    return jax.shard_map(device_step, mesh=mesh, in_specs=(row_spec, pos_spec, head_cols, head_cols, head_cols, head_rows, ff_cols, ff_cols, ff_rows, gain_spec, gain_spec), out_specs=(row_spec, cache_spec, cache_spec), check_vma=False)
```

profile of v0, /device:TPU:0, one launch (start us, length us, event | category | flops | bytes accessed | tf_op | source)
XLA Modules:
  0.0 3190.4 jit_solution(1753008236232819625)
XLA Ops:
  67.5 38.1 %while.24 = (s32[]{:T(128)}, bf16[4,512,1,2,256]{4,1,0,3,2:T(8,128)(2,1)S(1)}, s32[4]{0:T(128)S(1)}, bf16[3072,1,256]{2,0,1:T(8,128)(2,1)}, s32[]{:T(128)}, /*in...) while((s32[]{:T(128)}, ...), condition=%wide.region_4.5_spmd, body=%wide.region_1.4_spmd.sunk | while | flops 1633684480 | bytes 33070368 | solution.py:77
  116.6 626.7 %all-reduce.4 = bf16[2048,2304]{1,0:T(8,128)(2,1)} all-reduce(f32[2048,2304]{1,0:T(8,128)} %convolution_bitcast_fusion.1), channel_id=1, replica_groups=mesh['dp'=2,'tp'=4,'sp'=4] {'tp'}, use_global_device_ids=true, to_apply=%region_5.6 | all-reduce | flops 4718592 | bytes 28311552 | tf_op jit(solution)/shard_map/psum | solution.py:120
  755.4 27.7 fusion.78
  783.1 34.8 %multiply_convert_fusion.1 = bf16[2048,2304]{1,0:T(8,128)(2,1)} fusion(f32[2048,2304]{1,0:T(8,128)} %fusion.78, bf16[2,2304,2304]{2,1,0:T(8,128)(2,1)} %param.22, bf16[2048,2304]{1,0:T(8,128)(2,1)} %copy-done.3, f32[2304]{0:T(1024)S(1)} %get-tuple-element.210, f32[2048]{0:T(1024)S(1)} %add_rsqrt_fusion.2), kind=kOutput, calls=%fused_computation.80 | convolution fusion | flops 21790457856 | bytes 48382976 | tf_op jit(solution)/shard_map/dot_general | solution.py:124
  817.9 30.6 fusion.75
  848.6 625.7 %all-reduce.5 = bf16[2048,2304]{1,0:T(8,128)(2,1)} all-reduce(f32[2048,2304]{1,0:T(8,128)} %fusion.75), channel_id=1, replica_groups=mesh['dp'=2,'tp'=4,'sp'=4] {'tp'}, use_global_device_ids=true, to_apply=%region_7.8 | all-reduce | flops 4718592 | bytes 28311552 | tf_op jit(solution)/shard_map/psum | solution.py:127
  1535.5 29.7 all-gather.6.cloned.1.call-done
  1565.3 230.9 %while.25 = (s32[]{:T(128)}, bf16[4,512,1,2,256]{4,1,0,3,2:T(8,128)(2,1)S(1)}, s32[4]{0:T(128)S(1)}, s32[]{:T(128)}, bf16[2048,1,2,256]{0,3,2,1:T(8,128)(2,1)}, ...) while((s32[]{:T(128)}, ...), condition=%wide.region_12.13_spmd.clone.clone, body=%wide.region_9.12_spmd.clone.clone.sunk | while | flops 8699246592 | bytes 126902464 | solution.py:60
  1572.9 16.7 fusion.179
  1589.6 15.7 fusion.180
  1605.3 17.9 fusion.181
  1630.5 16.7 fusion.179
  1647.2 15.7 fusion.180
  1662.9 17.9 fusion.181
  1688.1 16.7 fusion.179
  1704.8 15.7 fusion.180
  1720.5 17.9 fusion.181
  1745.7 16.7 fusion.179
  1778.1 17.9 fusion.181
  1807.0 632.8 %all-reduce.6 = bf16[2048,2304]{1,0:T(8,128)(2,1)} all-reduce(f32[2048,2304]{1,0:T(8,128)} %convolution_bitcast_fusion), channel_id=1, replica_groups=mesh['dp'=2,'tp'=4,'sp'=4] {'tp'}, use_global_device_ids=true, to_apply=%region_13.14 | all-reduce | flops 4718592 | bytes 28311552 | tf_op jit(solution)/shard_map/psum | solution.py:120
  2451.9 27.7 fusion.73
  2479.6 34.6 %multiply_convert_fusion = bf16[2048,2304]{1,0:T(8,128)(2,1)} fusion(f32[2048,2304]{1,0:T(8,128)} %fusion.73, bf16[2,2304,2304]{2,1,0:T(8,128)(2,1)} %param.22, bf16[2048,2304]{1,0:T(8,128)(2,1)} %copy-done, f32[2304]{0:T(1024)S(1)} %copy-done.25, f32[2048]{0:T(1024)S(1)} %add_rsqrt_fusion), kind=kOutput, calls=%fused_computation.79 | convolution fusion | flops 21790457856 | bytes 48382976 | tf_op jit(solution)/shard_map/dot_general | solution.py:124
  2514.2 30.4 fusion.70
  2544.6 626.9 %all-reduce.7 = bf16[2048,2304]{1,0:T(8,128)(2,1)} all-reduce(f32[2048,2304]{1,0:T(8,128)} %fusion.70), channel_id=1, replica_groups=mesh['dp'=2,'tp'=4,'sp'=4] {'tp'}, use_global_device_ids=true, to_apply=%region_15.16 | all-reduce | flops 4718592 | bytes 28311552 | tf_op jit(solution)/shard_map/psum | solution.py:127
  (181 shorter events, 255.9 us)
Async XLA Ops:
  7.2 7.6 copy-start.27
  7.2 1521.9 %all-gather.4.cloned.1.call-start = ((), (), s32[]{:S(2)}) async-start(), calls=%async_computation | async-start | bytes 5242880 | tf_op jit(solution)/shard_map/all_gather | solution.py:116
  7.2 7.6 copy-start.1
  7.2 30.4 copy-start.28
  14.8 22.8 copy-start.22
  14.8 13.8 copy-start.31
  24.5 17.9 slice-start
  25.3 17.0 slice-start.1
  25.3 37.5 %collective-permute-start.1 = (bf16[1024,1,256]{0,2,1:T(8,128)(2,1)}, bf16[1024,1,256]{0,2,1:T(8,128)(2,1)}, u32[]{:S(2)}, u32[]{:S(2)}) collective-permute-start(bf16[1024,1,256]{0,2,1:T(8,128)(2,1)} %pad_maximum_fusion.5), channel_id=1, source_target_pairs={{0,1},{1,2},{2,3},{4,5},{5,6},{6,7},{8,9},{9,10},{10,11},{12,13},{... | collective-permute-start | bytes 1572872 | tf_op jit(solution)/shard_map/ppermute | solution.py:110
  31.7 6.0 copy-start.15
  32.6 32.5 %collective-permute-start = (bf16[1024,1,256]{2,0,1:T(8,128)(2,1)}, bf16[1024,1,256]{2,0,1:T(8,128)(2,1)}, u32[]{:S(2)}, u32[]{:S(2)}) collective-permute-start(bf16[1024,1,256]{2,0,1:T(8,128)(2,1)} %slice_bitcast_fusion), channel_id=1, source_target_pairs={{0,1},{1,2},{2,3},{4,5},{5,6},{6,7},{8,9},{9,10},{10,11},{12,13},{... | collective-permute-start | bytes 1572872 | tf_op jit(solution)/shard_map/ppermute | solution.py:111
  42.4 17.4 copy-start.5
  51.1 8.7 copy-start.7
  59.8 5.3 copy-start.16
  98.8 4.3 copy-start.21
  1474.3 8.5 copy-start.26
  1474.3 8.5 copy-start.30
  1492.8 8.2 copy-start.4
  1492.8 12.8 copy-start.11
  1492.8 12.8 copy-start.14
  1492.8 72.4 %all-gather.6.cloned.1.call-start = ((), (), s32[]{:S(2)}) async-start(), calls=%async_computation.1 | async-start | bytes 5242880 | tf_op jit(solution)/shard_map/all_gather | solution.py:117
  1509.4 8.7 copy-start.6
  1509.4 8.7 copy-start.8
  2439.8 12.1 copy-start.25
  (17 other events, 48.9 us)
Sparse Core Ops, SparseCore 0:
  1492.9 36.1 all-gather.3
  1530.6 34.4 all-gather.5
where the time goes:
time: 3200 us; the launch traced here: 3190 us
  blocking collectives  2510 us (78%)
  matrix products  403 us (13%)
  other arithmetic  170 us (5%)
  local copies, waits for them, and re-layouts  39.5 us (1%)
  waiting for transfers between devices  36.8 us (1%)
    psum x2, blocking collectives, device_step(): attn_sum = lax.psum(attn_part, 'tp').astype(jnp.bfloat16)  1260 us
    psum x2, blocking collectives, device_step(): mlp_sum = lax.psum(mlp_part, 'tp').astype(jnp.bfloat16)  1250 us
    dot_general x8, matrix products, attend_rows(): jnp.einsum('tkgs,skd->tkgd', probs_bf, v_rows, preferred_element_type=jnp...  80.9 us
    dot_general x8, matrix products, attend_rows(): jnp.einsum('tkgd,skd->tkgs', q_rows, k_rows, preferred_element_type=jnp.f...  77.9 us
    dot_general x2, matrix products, device_step(): jnp.dot(normed, w_up[layer_id], preferred_element_type=jnp.float32)  69.4 us
    reduce_sum x8, other arithmetic, softmax_rows(): jnp.sum(weights, axis=-1, keepdims=True)  68.8 us
  transfers between devices with their start and end apart: 4, of which 2 were waited for; matrix products, arithmetic and copies ran while one was open for 2% of the time, Pallas kernels for 0%

commit v1 on v0

v1 whole, which is shorter than its diff:
```python
import functools

import jax
import jax.numpy as jnp
from jax import lax
from jax.experimental import pallas as pl
from jax.experimental.pallas import tpu as pltpu
from jax.sharding import PartitionSpec as P


ROPE_BASE = 10000.0
NORM_EPS = 1e-6
WINDOW = 1024
HEAD = 256
HALF = 128
TQ = 512
TW = 256
EXP_SCALE = (HEAD ** -0.5) * 1.4426950408889634
NEG = -1.6e31
F32 = jnp.float32
BF16 = jnp.bfloat16


def rms_norm(hidden, gain_vec):
    hidden_f = hidden.astype(F32)
    inv_rms = lax.rsqrt(jnp.mean(hidden_f * hidden_f, axis=-1, keepdims=True) + NORM_EPS)
    return (hidden_f * inv_rms * gain_vec.astype(F32)).astype(BF16)


def rope_tables(positions):
    inv_freq = ROPE_BASE ** (-2.0 * jnp.arange(HALF, dtype=F32) / HEAD)
    angles = positions.astype(F32)[:, None] * inv_freq[None, :]
    return jnp.cos(angles), jnp.sin(angles)


def rotate(vals, cosine, sine, num_heads):
    parts = []
    for h in range(num_heads):
        a = vals[..., h * HEAD:h * HEAD + HALF].astype(F32)
        b = vals[..., h * HEAD + HALF:(h + 1) * HEAD].astype(F32)
        parts.append((a * cosine - b * sine).astype(BF16))
        parts.append((b * cosine + a * sine).astype(BF16))
    parts.append(vals[..., num_heads * HEAD:])
    return jnp.concatenate(parts, axis=-1)


def dot32(a, b):
    return jnp.dot(a, b, preferred_element_type=F32)


def raw_scores(q, k):
    return lax.dot_general(q, k, (((1,), (1,)), ((), ())), preferred_element_type=F32)


def window_kernel(c_ref, q_ref, kv_ref, o_ref):
    i = pl.program_id(0)
    span = WINDOW + TW
    base = pl.multiple_of(i * TW, TW)
    k = kv_ref[pl.ds(base, span), :HEAD]
    v = kv_ref[pl.ds(base, span), HEAD:]
    row = lax.broadcasted_iota(jnp.int32, (TW, span), 0)
    col = lax.broadcasted_iota(jnp.int32, (TW, span), 1)
    first = jnp.where(c_ref[0] > 0, 0, WINDOW - i * TW)
    visible = (col <= row + WINDOW) & (col >= row) & (col >= first)
    for h in range(2):
        s = raw_scores(q_ref[:, h * HEAD:(h + 1) * HEAD], k)
        s = jnp.where(visible, s, NEG)
        e = jnp.exp2((s - jnp.max(s, axis=-1, keepdims=True)) * EXP_SCALE)
        p = (e / jnp.sum(e, axis=-1, keepdims=True)).astype(BF16)
        o_ref[:, h * HEAD:(h + 1) * HEAD] = dot32(p, v).astype(BF16)


def window_attention(c, q, kv_ext):
    num = q.shape[0]
    return pl.pallas_call(
        window_kernel,
        out_shape=jax.ShapeDtypeStruct((num, 2 * HEAD), BF16),
        grid_spec=pltpu.PrefetchScalarGridSpec(
            num_scalar_prefetch=1,
            grid=(num // TW,),
            in_specs=[
                pl.BlockSpec((TW, 2 * HEAD), lambda i, c: (i, 0)),
                pl.BlockSpec(kv_ext.shape, lambda i, c: (0, 0)),
            ],
            out_specs=pl.BlockSpec((TW, 2 * HEAD), lambda i, c: (i, 0)),
        ),
        compiler_params=pltpu.CompilerParams(vmem_limit_bytes=40 * 2**20),
        cost_estimate=pl.CostEstimate(flops=8 * num * (WINDOW + TW) * HEAD, bytes_accessed=num * HEAD * 14, transcendentals=0),
        name="window_attn",
    )(c, q, kv_ext)


def causal_kernel(c_ref, q_ref, kl_ref, *refs):
    pieces = refs[0:2], refs[2:4], refs[4:6]
    o_ref, m_ref, l_ref, acc_ref, join_ref = refs[6:]
    i = pl.program_id(0)
    num = kl_ref.shape[0]
    c = c_ref[0]
    m_ref[...] = jnp.full(m_ref.shape, NEG, F32)
    l_ref[...] = jnp.zeros(l_ref.shape, F32)
    acc_ref[...] = jnp.zeros(acc_ref.shape, F32)

    @pl.when(i == 0)
    def _():
        for g, (a_ref, b_ref) in enumerate(pieces):
            split = a_ref.shape[0]
            join_ref[g, :split] = a_ref[...]
            join_ref[g, split:] = b_ref[...]

    def block(kv_ref, start, size, diagonal):
        start = pl.multiple_of(start, size)
        k = kv_ref[pl.ds(start, size), :HEAD]
        v = kv_ref[pl.ds(start, size), HEAD:]
        logits = [raw_scores(q_ref[:, h * HEAD:(h + 1) * HEAD], k) for h in range(2)]
        for h in range(2):
            s = logits[h]
            if diagonal:
                row = lax.broadcasted_iota(jnp.int32, s.shape, 0)
                col = lax.broadcasted_iota(jnp.int32, s.shape, 1)
                s = jnp.where(col <= row, s, NEG)
            m_old = m_ref[h]
            m_new = jnp.maximum(m_old, jnp.max(s, axis=-1, keepdims=True))
            scale = jnp.exp2((m_old - m_new) * EXP_SCALE)
            e = jnp.exp2((s - m_new[:, :1]) * EXP_SCALE)
            part = e[:, :HALF]
            for g in range(1, size // HALF):
                part = part + e[:, g * HALF:(g + 1) * HALF]
            l_ref[h] = l_ref[h] * scale + part
            m_ref[h] = m_new
            acc_ref[h] = acc_ref[h] * scale[:, :1] + dot32(e.astype(BF16), v)

    def sweep(kv_ref, lo, hi, size):
        def body(j, carry):
            block(kv_ref, j * size, size, False)
            return carry

        lax.fori_loop(lo, hi, body, 0)

    block(kl_ref, i * TQ, TQ, True)
    sweep(kl_ref, 0, i, TQ)
    for g, seen in enumerate((c % 2 == 1, c >= 2, c >= 2)):
        @pl.when(seen)
        def _(g=g):
            block(join_ref.at[g], 0, num, False)
    for h in range(2):
        total = jnp.sum(l_ref[h], axis=-1, keepdims=True)
        o_ref[:, h * HEAD:(h + 1) * HEAD] = (acc_ref[h] / total).astype(BF16)


def causal_attention(c, q, kvs):
    num = q.shape[0]
    full = [pl.BlockSpec(kv.shape, lambda i, c: (0, 0)) for kv in kvs]
    return pl.pallas_call(
        causal_kernel,
        out_shape=jax.ShapeDtypeStruct((num, 2 * HEAD), BF16),
        grid_spec=pltpu.PrefetchScalarGridSpec(
            num_scalar_prefetch=1,
            grid=(num // TQ,),
            in_specs=[pl.BlockSpec((TQ, 2 * HEAD), lambda i, c: (i, 0))] + full,
            out_specs=pl.BlockSpec((TQ, 2 * HEAD), lambda i, c: (i, 0)),
            scratch_shapes=[
                pltpu.VMEM((2, TQ, HALF), F32),
                pltpu.VMEM((2, TQ, HALF), F32),
                pltpu.VMEM((2, TQ, HEAD), F32),
                pltpu.VMEM((3, num, 2 * HEAD), BF16),
            ],
        ),
        compiler_params=pltpu.CompilerParams(vmem_limit_bytes=56 * 2**20),
        cost_estimate=pl.CostEstimate(flops=8 * num * 4 * num * HEAD, bytes_accessed=num * HEAD * 20, transcendentals=0),
        name="causal_attn",
    )(c, q, *kvs)


def ff_kernel(has_init, h_ref, g_ref, u_ref, d_ref, *rest):
    o_ref = rest[-1]
    n = pl.program_id(0)
    h = h_ref[...]
    g = dot32(h, g_ref[...].reshape(g_ref.shape[-2:]))
    u = dot32(h, u_ref[...].reshape(u_ref.shape[-2:]))
    act = (jax.nn.silu(g) * u).astype(BF16)
    d = d_ref[...].reshape(d_ref.shape[-2:])

    @pl.when(n == 0)
    def _():
        first = dot32(act, d)
        o_ref[...] = rest[0][...] + first if has_init else first

    @pl.when(n > 0)
    def _():
        o_ref[...] += dot32(act, d)


def ff_part(h, weights, init=None):
    g, u, d, layer = weights
    rows, width = h.shape
    if layer is None:
        ff = d.shape[0]
        tn = 384 if ff % 768 else (768 if rows <= 256 else 256)
        shift = ff // tn if u is g else 0
        gate = pl.BlockSpec((width, tn), lambda n: (0, n))
        up = pl.BlockSpec((width, tn), lambda n: (0, n + shift))
        down = pl.BlockSpec((tn, width), lambda n: (n, 0))
    else:
        ff = d.shape[1]
        tn = 768 if rows <= 256 else 256
        gate = up = pl.BlockSpec((1, width, tn), lambda n: (layer, 0, n))
        down = pl.BlockSpec((1, tn, width), lambda n: (layer, n, 0))
    whole = pl.BlockSpec((rows, width), lambda n: (0, 0))
    extra = [] if init is None else [init]
    return pl.pallas_call(
        functools.partial(ff_kernel, init is not None),
        out_shape=jax.ShapeDtypeStruct((rows, width), F32),
        grid=(ff // tn,),
        in_specs=[whole, gate, up, down] + [whole] * len(extra),
        out_specs=whole,
        compiler_params=pltpu.CompilerParams(vmem_limit_bytes=56 * 2**20),
        cost_estimate=pl.CostEstimate(flops=6 * rows * width * ff, bytes_accessed=6 * width * ff, transcendentals=0),
        name="ff_part",
    )(h, g, u, d, *extra)


def solution(mesh):
    num_tp = mesh.shape['tp']
    num_sp = mesh.shape['sp']
    num_plane = mesh.shape['dp'] * num_sp
    row_spec = P(('dp', 'sp'), None)
    pos_spec = P(('dp', 'sp'))
    head_cols = P(None, None, 'tp', None)
    head_rows = P(None, 'tp', None, None)
    ff_cols = P(None, None, 'tp')
    ff_rows = P(None, 'tp', None)
    gain_spec = P(None, None)
    cache_spec = P(None, ('dp', 'sp'), 'tp', None)
    flip = {k: [(i, i ^ k) for i in range(num_tp)] for k in (1, 2, 3)}
    ring_up = [(i, (i + 1) % num_tp) for i in range(num_tp)]
    ring_dn = [(i, (i - 1) % num_tp) for i in range(num_tp)]
    sp_next = [(i, i + 1) for i in range(num_sp - 1)]
    sp_core = [(i, i ^ 1) for i in range(num_sp)]
    sp_far = [(i, i + 2) for i in range(2)]

    def layers(embeds, positions, w_query, w_key, w_value, w_out, w_gate, w_up, w_down, attn_gain, mlp_gain):
        num = embeds.shape[0]
        width = embeds.shape[1]
        own = num // num_tp
        z = lax.axis_index('tp')
        c = lax.axis_index('sp')
        seat = lax.axis_index('dp') * num_sp + c
        c_arr = c.astype(jnp.int32).reshape(1)
        ff = w_gate.shape[2]
        num_layers = w_gate.shape[0]
        heads_w = w_query.shape[2] * HEAD

        def gather_all(w):
            piece = lax.dynamic_index_in_dim(w.reshape(num_plane, -1, w.shape[-1]), seat, 0, keepdims=False)
            return lax.all_gather(piece, ('tp', 'dp', 'sp'), axis=0, tiled=True)

        def plane_gather(piece):
            return lax.all_gather(piece, ('dp', 'sp'), axis=0, tiled=True)

        def ff_pieces(layer_id, splits):
            cols = ff // splits
            rows, drows = width // num_plane, cols // num_plane
            sent = []
            for s in range(splits):
                view = (num_layers, num_plane, rows, ff)
                at = (layer_id, seat, 0, s * cols)
                g = lax.dynamic_slice(w_gate.reshape(view), at, (1, 1, rows, cols)).reshape(rows, cols)
                u = lax.dynamic_slice(w_up.reshape(view), at, (1, 1, rows, cols)).reshape(rows, cols)
                d = lax.dynamic_slice(
                    w_down.reshape(num_layers, splits * num_plane, drows, width),
                    (layer_id, s * num_plane + seat, 0, 0), (1, 1, drows, width)).reshape(drows, width)
                sent += [jnp.concatenate([g, u], axis=1), d]
            return sent

        def cross(piece):
            return lax.ppermute(piece, 'tp', flip[2])

        def qkv_weight(layer_id):
            return jnp.concatenate([
                w_query[layer_id].reshape(width, heads_w),
                w_key[layer_id].reshape(width, HEAD),
                w_value[layer_id].reshape(width, HEAD)], axis=1)

        def place(buf, piece, block):
            return lax.dynamic_update_slice(buf, piece[None], (block,) + (0,) * piece.ndim)

        def spread_heads(attn):
            blocks = attn.reshape(num_tp, own, heads_w)
            buf = jnp.zeros((own, num_tp * heads_w), BF16)
            for k in (2, 3, 1, 0):
                piece = lax.dynamic_index_in_dim(blocks, z ^ k, 0, keepdims=False)
                if k:
                    piece = lax.ppermute(piece, 'tp', flip[k])
                buf = lax.dynamic_update_slice(buf, piece, (0, (z ^ k) * heads_w))
            return buf

        def residual(x, mine, back):
            m = (mine + back).astype(BF16)
            return (x.astype(F32) + m.astype(F32)).astype(BF16)

        def local_ff(layer_id):
            return (w_gate, w_up, w_down, layer_id)

        half = own // 2
        sent0 = []
        for piece in ff_pieces(0, 2):
            sent0.append(cross(piece))
        cosine, sine = rope_tables(positions)

        normed0 = rms_norm(embeds, attn_gain[0])
        weight = qkv_weight(0)
        qkv = dot32(normed0, weight).astype(BF16)
        qkv = rotate(qkv, cosine, sine, 3)
        q0, kv0 = qkv[:, :heads_w], qkv[:, heads_w:]
        halo = lax.ppermute(kv0[num - WINDOW:], 'sp', sp_next)
        kv_ext = jnp.concatenate([halo, kv0], axis=0)
        attn0 = window_attention(c_arr, q0, kv_ext)
        wo0 = gather_all(w_out[0].reshape(heads_w, width))
        gu0 = plane_gather(sent0[0])
        d0 = plane_gather(sent0[1])
        gu1 = plane_gather(sent0[2])
        d1 = plane_gather(sent0[3])
        wo1 = gather_all(w_out[1].reshape(heads_w, width))
        x = lax.dynamic_index_in_dim(embeds.reshape(num_tp, own, width), z, 0, keepdims=False)
        o = dot32(spread_heads(attn0), wo0).astype(BF16)
        x = (x.astype(F32) + o.astype(F32)).astype(BF16)
        h2 = rms_norm(x, mlp_gain[0])
        theirs = lax.ppermute(h2, 'tp', flip[1])
        mine = ff_part(h2, local_ff(0))
        far_gu, far_d = ff_pieces(1, 1)
        far_gu = cross(far_gu)
        first, second = (gu0, gu0, d0, None), (gu1, gu1, d1, None)
        other = ff_part(theirs, local_ff(0))
        other = ff_part(theirs, first, other)
        mine = ff_part(h2, first, mine)
        outs = [ff_part(theirs[:half], second, other[:half])]
        outs.append(ff_part(theirs[half:], second, other[half:]))
        back = [lax.ppermute(out, 'tp', flip[1]) for out in outs]
        mine = ff_part(h2, second, mine)
        gu_far = plane_gather(far_gu)
        x = residual(x, mine, jnp.concatenate(back, axis=0))

        normed = rms_norm(x, attn_gain[1])
        weight = qkv_weight(1)
        cos_half = cosine.reshape(2 * num_tp, half, HALF)
        sin_half = sine.reshape(2 * num_tp, half, HALF)
        qkv1 = jnp.zeros((2 * num_tp, half, heads_w + 2 * HEAD), BF16)

        def project(rows, block):
            pick = functools.partial(lax.dynamic_index_in_dim, index=block, axis=0, keepdims=False)
            return rotate(dot32(rows, weight).astype(BF16), pick(cos_half), pick(sin_half), 3)

        def exchange(pieces):
            kv = jnp.concatenate([p[:, heads_w:] for p in pieces], axis=0)
            core = lax.ppermute(kv, 'sp', sp_core)
            far = lax.ppermute(kv, 'sp', sp_far)
            return core, far

        up, dn = normed[:half], normed[half:]
        done = []
        for s in range(num_tp):
            if s:
                up = lax.ppermute(up, 'tp', ring_up)
                dn = lax.ppermute(dn, 'tp', ring_dn)
            for rows, block in ((up, 2 * lax.rem(z - s + num_tp, num_tp)), (dn, 2 * lax.rem(z + s, num_tp) + 1)):
                out = project(rows, block)
                done.append(out)
                qkv1 = place(qkv1, out, block)
            if s == 2:
                core_a, far_a = exchange(done)
        core_b, far_b = exchange(done[6:])
        diag_a = lax.ppermute(far_a, 'sp', sp_core)
        diag_b = lax.ppermute(far_b, 'sp', sp_core)
        qkv1 = qkv1.reshape(num, heads_w + 2 * HEAD)
        q1, kv1 = qkv1[:, :heads_w], qkv1[:, heads_w:]
        far_d = cross(far_d)
        attn1 = causal_attention(c_arr, q1, (kv1, core_a, core_b, far_a, far_b, diag_a, diag_b))
        d_far = plane_gather(far_d)
        o = dot32(spread_heads(attn1), wo1).astype(BF16)
        x = (x.astype(F32) + o.astype(F32)).astype(BF16)
        h2 = rms_norm(x, mlp_gain[1])
        fetched = (gu_far, gu_far, d_far, None)
        theirs = [lax.ppermute(h2[s * half:(s + 1) * half], 'tp', flip[1]) for s in range(2)]
        out = ff_part(theirs[0], local_ff(1))
        out = ff_part(theirs[0], fetched, out)
        back = [lax.ppermute(out, 'tp', flip[1])]
        out = ff_part(theirs[1], local_ff(1))
        out = ff_part(theirs[1], fetched, out)
        back.append(lax.ppermute(out, 'tp', flip[1]))
        mine = ff_part(h2, fetched, ff_part(h2, local_ff(1)))
        x = residual(x, mine, jnp.concatenate(back, axis=0))

        up, dn = x[:half], x[half:]
        hidden = normed0.reshape(2 * num_tp, half, width)
        hidden = place(place(hidden, up, 2 * z), dn, 2 * z + 1)
        for s in range(1, num_tp):
            up = lax.ppermute(up, 'tp', ring_up)
            dn = lax.ppermute(dn, 'tp', ring_dn)
            hidden = place(hidden, up, 2 * lax.rem(z - s + num_tp, num_tp))
            hidden = place(hidden, dn, 2 * lax.rem(z + s, num_tp) + 1)
        kv = jnp.stack([kv0, kv1])[:, :, None, :]
        return hidden.reshape(num, width), kv[..., :HEAD], kv[..., HEAD:]


    return jax.shard_map(layers, mesh=mesh, in_specs=(row_spec, pos_spec, head_cols, head_cols, head_cols, head_rows, ff_cols, ff_cols, ff_rows, gain_spec, gain_spec), out_specs=(row_spec, cache_spec, cache_spec), check_vma=False)
```

time: 3200 us -> 1500 us (0.47)
  the two profiles are of different devices: /device:TPU:0 before, /device:TPU:7 now
where the time goes in v1:
time: 1500 us; the launch traced here: 1490 us
  waiting for transfers between devices  899 us (60%)
  Pallas kernels  342 us (23%)
  local copies, waits for them, and re-layouts  77.2 us (5%)
  matrix products  56 us (4%)
  other arithmetic  51.7 us (3%)
  starting transfers between devices  49.6 us (3%)
  between operations  15.3 us (1%)
    ppermute x6, waiting for transfers between devices, cross(): return lax.ppermute(piece, 'tp', flip[2])  283 us
    pallas_call x13, Pallas kernels, ff_part(): pl.pallas_call(functools.partial(ff_kernel, init is not None), out_shape=...  268 us
    ppermute x6, waiting for transfers between devices, spread_heads(): piece = lax.ppermute(piece, 'tp', flip[k])  167 us
    ppermute x6, waiting for transfers between devices, layers(): dn = lax.ppermute(dn, 'tp', ring_dn)  154 us
    ppermute x6, waiting for transfers between devices, layers(): up = lax.ppermute(up, 'tp', ring_up)  114 us
    pallas_call x1, Pallas kernels, causal_attention(): pl.pallas_call(causal_kernel, out_shape=jax.ShapeDtypeStruct((num, 2 * HE...  60.8 us
    dot_general x11, matrix products, dot32(): return jnp.dot(a, b, preferred_element_type=F32)  56 us
    ppermute x1, waiting for transfers between devices, layers(): theirs = lax.ppermute(h2, 'tp', flip[1])  54.7 us
  transfers between devices with their start and end apart: 46, of which 26 were waited for; matrix products, arithmetic and copies ran while one was open for 11% of the time, Pallas kernels for 22%

profile of v1, /device:TPU:7, one launch (start us, length us, event | category | flops | bytes accessed | tf_op | source)
XLA Modules:
  0.0 1490.7 jit_solution(12061512268180724164)
XLA Ops:
  17.6 35.0 %collective-permute-done.7 = bf16[144,2304]{1,0:T(8,128)(2,1)S(1)} collective-permute-done((bf16[144,2304]{1,0:T(8,128)(2,1)S(1)}, bf16[144,2304]{1,0:T(8,128)(2,1)S(1)}, u32[]{:S(2)}, u32[]{:S(2)}) %collective-permute-start.7) | collective-permute-done | bytes 663584 | tf_op jit(solution)/shard_map/ppermute | solution.py:276
  56.4 71.3 %collective-permute-done.6 = bf16[288,2304]{1,0:T(8,128)(2,1)} collective-permute-done((bf16[288,2304]{1,0:T(8,128)(2,1)S(1)}, bf16[288,2304]{1,0:T(8,128)(2,1)}, u32[]{:S(2)}, u32[]{:S(2)}) %collective-permute-start.6) | collective-permute-done | bytes 1327136 | tf_op jit(solution)/shard_map/ppermute | solution.py:276
  127.8 57.2 %collective-permute-done.5 = bf16[144,2304]{1,0:T(8,128)(2,1)} collective-permute-done((bf16[144,2304]{1,0:T(8,128)(2,1)}, bf16[144,2304]{1,0:T(8,128)(2,1)}, u32[]{:S(2)}, u32[]{:S(2)}) %collective-permute-start.5) | collective-permute-done | bytes 663584 | tf_op jit(solution)/shard_map/ppermute | solution.py:276
  186.4 59.6 %collective-permute-done.4 = bf16[288,2304]{1,0:T(8,128)(2,1)} collective-permute-done((bf16[288,2304]{1,0:T(8,128)(2,1)S(1)}, bf16[288,2304]{1,0:T(8,128)(2,1)}, u32[]{:S(2)}, u32[]{:S(2)}) %collective-permute-start.4) | collective-permute-done | bytes 1327136 | tf_op jit(solution)/shard_map/ppermute | solution.py:276
  248.3 59.8 %collective-permute-done.27 = bf16[288,2304]{1,0:T(8,128)(2,1)S(1)} collective-permute-done((bf16[288,2304]{1,0:T(8,128)(2,1)S(1)}, bf16[288,2304]{1,0:T(8,128)(2,1)S(1)}, u32[]{:S(2)}, u32[]{:S(2)}) %collective-permute-start.27) | collective-permute-done | bytes 1327136 | tf_op jit(solution)/shard_map/ppermute | solution.py:276
  387.3 143.9 %collective-permute-done.1 = bf16[512,512]{1,0:T(8,128)(2,1)} collective-permute-done((bf16[512,512]{1,0:T(8,128)(2,1)}, bf16[512,512]{1,0:T(8,128)(2,1)}, u32[]{:S(2)}, u32[]{:S(2)}) %collective-permute-start.1) | collective-permute-done | bytes 524320 | tf_op jit(solution)/shard_map/ppermute | solution.py:293
  563.5 54.7 %collective-permute-done.8.h_ref = bf16[512,2304]{1,0:T(8,128)(2,1)S(1)} collective-permute-done((bf16[512,2304]{1,0:T(8,128)(2,1)S(1)}, bf16[512,2304]{1,0:T(8,128)(2,1)S(1)}, u32[]{:S(2)}, u32[]{:S(2)}) %collective-permute-start.8) | collective-permute-done | bytes 2359328 | tf_op jit(solution)/shard_map/ppermute | solution.py:328
  619.6 26.0 %ff_part.16.rest_0_ = f32[512,2304]{1,0:T(8,128)} custom-call(bf16[512,2304]{1,0:T(8,128)(2,1)} %copy-done.2, bf16[2,2304,2304]{2,1,0:T(8,128)(2,1)} %g_ref.9, bf16[2,2304,2304]{2,1,0:T(8,128)(2,1)} %u_ref.9, bf16[2,2304,2304]{2,1,0:T(8,128)(2,1)} %d_ref.9), custom_call_target="tpu_custom_call" | custom-call | flops 16307453952 | bytes 31850496 | tf_op jit(solution)/shard_map/ff_part/pallas_call | solution.py:210
  645.6 22.4 %ff_part.17 = f32[512,2304]{1,0:T(8,128)} custom-call(bf16[512,2304]{1,0:T(8,128)(2,1)} %copy-done.2, bf16[2304,2304]{1,0:T(8,128)(2,1)} %all-gather.15.cloned.1.call-done.g_ref.u_ref, bf16[2304,2304]{1,0:T(8,128)(2,1)} %all-gather.15.cloned.1.call-done.g_ref.u_ref, bf16[1152,2304]{1,0:T(8,128)(2,1)} %all-gather.17.cloned.1.call-done.d_ref, ...), custom_call_target="tpu_custom_call" | custom-call | flops 8153726976 | bytes 15925248 | tf_op jit(solution)/shard_map/ff_part/pallas_call | solution.py:210
  702.8 26.1 %ff_part.13.rest_0_ = f32[512,2304]{1,0:T(8,128)} custom-call(bf16[512,2304]{1,0:T(8,128)(2,1)} %copy-done, bf16[2,2304,2304]{2,1,0:T(8,128)(2,1)} %g_ref.9, bf16[2,2304,2304]{2,1,0:T(8,128)(2,1)} %u_ref.9, bf16[2,2304,2304]{2,1,0:T(8,128)(2,1)} %d_ref.9), custom_call_target="tpu_custom_call" | custom-call | flops 16307453952 | bytes 31850496 | tf_op jit(solution)/shard_map/ff_part/pallas_call | solution.py:210
  824.5 23.2 %collective-permute-done.12 = bf16[256,2304]{1,0:T(8,128)(2,1)} collective-permute-done((bf16[256,2304]{1,0:T(8,128)(2,1)}, bf16[256,2304]{1,0:T(8,128)(2,1)}, u32[]{:S(2)}, u32[]{:S(2)}) %collective-permute-start.12) | collective-permute-done | bytes 1179680 | tf_op jit(solution)/shard_map/ppermute | solution.py:364
  874.4 27.5 %collective-permute-done.14 = bf16[256,2304]{1,0:T(8,128)(2,1)S(1)} collective-permute-done((bf16[256,2304]{1,0:T(8,128)(2,1)}, bf16[256,2304]{1,0:T(8,128)(2,1)S(1)}, u32[]{:S(2)}, u32[]{:S(2)}) %collective-permute-start.14) | collective-permute-done | bytes 1179680 | tf_op jit(solution)/shard_map/ppermute | solution.py:364
  927.6 24.9 %collective-permute-done.16 = bf16[256,2304]{1,0:T(8,128)(2,1)S(1)} collective-permute-done((bf16[256,2304]{1,0:T(8,128)(2,1)S(1)}, bf16[256,2304]{1,0:T(8,128)(2,1)S(1)}, u32[]{:S(2)}, u32[]{:S(2)}) %collective-permute-start.16) | collective-permute-done | bytes 1179680 | tf_op jit(solution)/shard_map/ppermute | solution.py:364
  960.9 37.8 %collective-permute-done.19.refs_2_ = bf16[1536,512]{1,0:T(8,128)(2,1)S(1)} collective-permute-done((bf16[1536,512]{1,0:T(8,128)(2,1)S(1)}, bf16[1536,512]{1,0:T(8,128)(2,1)S(1)}, u32[]{:S(2)}, u32[]{:S(2)}) %collective-permute-start.19) | collective-permute-done | bytes 1572896 | tf_op jit(solution)/shard_map/ppermute | solution.py:356
  1016.1 60.8 %causal_attn.1 = bf16[2048,512]{1,0:T(8,128)(2,1)} custom-call(s32[1]{0:T(128)} %bitcast.3.c_ref, bf16[2048,512]{1,0:T(8,128)(2,1)} %get-tuple-element.66.q_ref, bf16[2048,512]{1,0:T(8,128)(2,1)} %get-tuple-element.65.kl_ref, bf16[1536,512]{1,0:T(8,128)(2,1)} %copy-done.28, bf16[512,512]{1,0:T(8,128)(2,1)} %copy-done.31, bf16[1536,512]{1,0:T(8,128)(2,1)} %copy-done.27, ...), custom_call_target="tpu_custom_call" | custom-call | flops 34359738368 | bytes 10485760 | tf_op jit(solution)/shard_map/causal_attn/pallas_call | solution.py:153
  1081.1 23.1 %collective-permute-done.23 = bf16[512,512]{1,0:T(8,128)(2,1)S(1)} collective-permute-done((bf16[512,512]{1,0:T(8,128)(2,1)S(1)}, bf16[512,512]{1,0:T(8,128)(2,1)S(1)}, u32[]{:S(2)}, u32[]{:S(2)}) %collective-permute-start.23) | collective-permute-done | bytes 524320 | tf_op jit(solution)/shard_map/ppermute | solution.py:293
  1240.1 25.7 %ff_part.20.rest_0_ = f32[512,2304]{1,0:T(8,128)} custom-call(bf16[512,2304]{1,0:T(8,128)(2,1)} %copy-done.1, bf16[2,2304,2304]{2,1,0:T(8,128)(2,1)} %g_ref.9, bf16[2,2304,2304]{2,1,0:T(8,128)(2,1)} %u_ref.9, bf16[2,2304,2304]{2,1,0:T(8,128)(2,1)} %d_ref.9), custom_call_target="tpu_custom_call" | custom-call | flops 16307453952 | bytes 31850496 | tf_op jit(solution)/shard_map/ff_part/pallas_call | solution.py:210
  1265.7 27.2 %ff_part.21 = f32[512,2304]{1,0:T(8,128)} custom-call(bf16[512,2304]{1,0:T(8,128)(2,1)} %copy-done.1, bf16[2304,4608]{1,0:T(8,128)(2,1)} %all-gather.19.cloned.1.call-done.g_ref.u_ref, bf16[2304,4608]{1,0:T(8,128)(2,1)} %all-gather.19.cloned.1.call-done.g_ref.u_ref, bf16[2304,2304]{1,0:T(8,128)(2,1)} %all-gather.21.cloned.1.call-done.d_ref, ...), custom_call_target="tpu_custom_call" | custom-call | flops 16307453952 | bytes 31850496 | tf_op jit(solution)/shard_map/ff_part/pallas_call | solution.py:210
  1292.9 30.1 %collective-permute-done.31 = f32[256,2304]{1,0:T(8,128)S(1)} collective-permute-done((f32[256,2304]{1,0:T(8,128)}, f32[256,2304]{1,0:T(8,128)S(1)}, u32[]{:S(2)}, u32[]{:S(2)}) %collective-permute-start.31) | collective-permute-done | bytes 2359328 | tf_op jit(solution)/shard_map/ppermute | solution.py:389
  1331.8 22.3 %collective-permute-done.32 = bf16[256,2304]{1,0:T(8,128)(2,1)S(1)} collective-permute-done((bf16[256,2304]{1,0:T(8,128)(2,1)S(1)}, bf16[256,2304]{1,0:T(8,128)(2,1)S(1)}, u32[]{:S(2)}, u32[]{:S(2)}) %collective-permute-start.32) | collective-permute-done | bytes 1179680 | tf_op jit(solution)/shard_map/ppermute | solution.py:397
  1354.0 25.7 %collective-permute-done.33 = bf16[256,2304]{1,0:T(8,128)(2,1)S(1)} collective-permute-done((bf16[256,2304]{1,0:T(8,128)(2,1)S(1)}, bf16[256,2304]{1,0:T(8,128)(2,1)S(1)}, u32[]{:S(2)}, u32[]{:S(2)}) %collective-permute-start.33) | collective-permute-done | bytes 1179680 | tf_op jit(solution)/shard_map/ppermute | solution.py:398
  1382.1 22.6 %collective-permute-done.34 = bf16[256,2304]{1,0:T(8,128)(2,1)S(1)} collective-permute-done((bf16[256,2304]{1,0:T(8,128)(2,1)S(1)}, bf16[256,2304]{1,0:T(8,128)(2,1)S(1)}, u32[]{:S(2)}, u32[]{:S(2)}) %collective-permute-start.34) | collective-permute-done | bytes 1179680 | tf_op jit(solution)/shard_map/ppermute | solution.py:397
  1404.6 26.9 %collective-permute-done.35 = bf16[256,2304]{1,0:T(8,128)(2,1)S(1)} collective-permute-done((bf16[256,2304]{1,0:T(8,128)(2,1)S(1)}, bf16[256,2304]{1,0:T(8,128)(2,1)S(1)}, u32[]{:S(2)}, u32[]{:S(2)}) %collective-permute-start.35) | collective-permute-done | bytes 1179680 | tf_op jit(solution)/shard_map/ppermute | solution.py:398
  1456.4 26.2 %collective-permute-done.37 = bf16[256,2304]{1,0:T(8,128)(2,1)S(1)} collective-permute-done((bf16[256,2304]{1,0:T(8,128)(2,1)S(1)}, bf16[256,2304]{1,0:T(8,128)(2,1)S(1)}, u32[]{:S(2)}, u32[]{:S(2)}) %collective-permute-start.37) | collective-permute-done | bytes 1179680 | tf_op jit(solution)/shard_map/ppermute | solution.py:398
  (269 shorter events, 515.7 us)
Async XLA Ops:
  7.2 529.1 %all-gather.23.cloned.1.call-start = ((), (), s32[]{:S(2)}) async-start(), calls=%async_computation.6 | async-start | bytes 9732096 | tf_op jit(solution)/shard_map/all_gather | solution.py:255
  13.0 632.6 %all-gather.17.cloned.1.call-start = ((), (), s32[]{:S(2)}) async-start(), calls=%async_computation.3 | async-start | bytes 5971968 | tf_op jit(solution)/shard_map/all_gather | solution.py:258
  53.5 592.2 %all-gather.15.cloned.1.call-start = ((), (), s32[]{:S(2)}) async-start(), calls=%async_computation.2 | async-start | bytes 11943936 | tf_op jit(solution)/shard_map/all_gather | solution.py:258
  56.4 71.3 %collective-permute-start.6 = (bf16[288,2304]{1,0:T(8,128)(2,1)S(1)}, bf16[288,2304]{1,0:T(8,128)(2,1)}, u32[]{:S(2)}, u32[]{:S(2)}) collective-permute-start(bf16[288,2304]{1,0:T(8,128)(2,1)S(1)} %pad_maximum_fusion.5), channel_id=1, source_target_pairs={{0,8},{4,12},{8,0},{12,4},{1,9},{5,13},{9,1},{13,5},{2,10},{6,14},... | collective-permute-start | bytes 3981320 | tf_op jit(solution)/shard_map/ppermute | solution.py:276
  127.7 546.0 %all-gather.13.cloned.1.call-start = ((), (), s32[]{:S(2)}) async-start(), calls=%async_computation.1 | async-start | bytes 5971968 | tf_op jit(solution)/shard_map/all_gather | solution.py:258
  127.8 57.3 %collective-permute-start.5 = (bf16[144,2304]{1,0:T(8,128)(2,1)}, bf16[144,2304]{1,0:T(8,128)(2,1)}, u32[]{:S(2)}, u32[]{:S(2)}) collective-permute-start(bf16[144,2304]{1,0:T(8,128)(2,1)} %get-tuple-element.45), channel_id=1, source_target_pairs={{0,8},{4,12},{8,0},{12,4},{1,9},{5,13},{9,1},{13,5},{2,10},{6,14},... | collective-permute-start | bytes 1990664 | tf_op jit(solution)/shard_map/ppermute | solution.py:276
  185.0 488.7 %all-gather.11.cloned.1.call-start = ((), (), s32[]{:S(2)}) async-start(), calls=%async_computation | async-start | bytes 11943936 | tf_op jit(solution)/shard_map/all_gather | solution.py:258
  186.3 59.6 %collective-permute-start.4 = (bf16[288,2304]{1,0:T(8,128)(2,1)S(1)}, bf16[288,2304]{1,0:T(8,128)(2,1)}, u32[]{:S(2)}, u32[]{:S(2)}) collective-permute-start(bf16[288,2304]{1,0:T(8,128)(2,1)S(1)} %pad_maximum_fusion.4), channel_id=1, source_target_pairs={{0,8},{4,12},{8,0},{12,4},{1,9},{5,13},{9,1},{13,5},{2,10},{6,14},... | collective-permute-start | bytes 3981320 | tf_op jit(solution)/shard_map/ppermute | solution.py:276
  246.0 864.2 %all-gather.25.cloned.1.call-start = ((), (), s32[]{:S(2)}) async-start(), calls=%async_computation.7 | async-start | bytes 9732096 | tf_op jit(solution)/shard_map/all_gather | solution.py:255
  246.8 954.9 %all-gather.21.cloned.1.call-start = ((), (), s32[]{:S(2)}) async-start(), calls=%async_computation.5 | async-start | bytes 11943936 | tf_op jit(solution)/shard_map/all_gather | solution.py:258
  248.3 59.9 %collective-permute-start.27 = (bf16[288,2304]{1,0:T(8,128)(2,1)S(1)}, bf16[288,2304]{1,0:T(8,128)(2,1)S(1)}, u32[]{:S(2)}, u32[]{:S(2)}) collective-permute-start(bf16[288,2304]{1,0:T(8,128)(2,1)S(1)} %dynamic-slice_bitcast_fusion), channel_id=1, source_target_pairs={{0,8},{4,12},{8,0},{12,4},{1,9},{5,13},{9,1},{13,5},{2,10},{6,14},... | collective-permute-start | bytes 3981320 | tf_op jit(solution)/shard_map/ppermute | solution.py:276
  309.4 892.4 %all-gather.19.cloned.1.call-start = ((), (), s32[]{:S(2)}) async-start(), calls=%async_computation.4 | async-start | bytes 23887872 | tf_op jit(solution)/shard_map/all_gather | solution.py:258
  362.4 173.8 %collective-permute-start.26 = (bf16[288,4608]{1,0:T(8,128)(2,1)}, bf16[288,4608]{1,0:T(8,128)(2,1)}, u32[]{:S(2)}, u32[]{:S(2)}) collective-permute-start(bf16[288,4608]{1,0:T(8,128)(2,1)} %pad_maximum_fusion.1), channel_id=1, source_target_pairs={{0,8},{4,12},{8,0},{12,4},{1,9},{5,13},{9,1},{13,5},{2,10},{6,14},... | collective-permute-start | bytes 7962632 | tf_op jit(solution)/shard_map/ppermute | solution.py:276
  383.4 147.8 %collective-permute-start.1 = (bf16[512,512]{1,0:T(8,128)(2,1)}, bf16[512,512]{1,0:T(8,128)(2,1)}, u32[]{:S(2)}, u32[]{:S(2)}) collective-permute-start(bf16[512,512]{1,0:T(8,128)(2,1)} %get-tuple-element.143), channel_id=1, source_target_pairs={{0,8},{4,12},{8,0},{12,4},{1,9},{5,13},{9,1},{13,5},{2,10},{6,14},... | collective-permute-start | bytes 1572872 | tf_op jit(solution)/shard_map/ppermute | solution.py:293
  385.8 146.8 %collective-permute-start.2 = (bf16[512,512]{1,0:T(8,128)(2,1)S(1)}, bf16[512,512]{1,0:T(8,128)(2,1)}, u32[]{:S(2)}, u32[]{:S(2)}) collective-permute-start(bf16[512,512]{1,0:T(8,128)(2,1)S(1)} %get-tuple-element.142), channel_id=1, source_target_pairs={{0,12},{4,8},{8,4},{12,0},{1,13},{5,9},{9,5},{13,1},{2,14},{6,10},... | collective-permute-start | bytes 1572872 | tf_op jit(solution)/shard_map/ppermute | solution.py:293
  386.7 147.0 %collective-permute-start.3 = (bf16[512,512]{1,0:T(8,128)(2,1)S(1)}, bf16[512,512]{1,0:T(8,128)(2,1)}, u32[]{:S(2)}, u32[]{:S(2)}) collective-permute-start(bf16[512,512]{1,0:T(8,128)(2,1)S(1)} %get-tuple-element.141), channel_id=1, source_target_pairs={{0,4},{4,0},{8,12},{12,8},{1,5},{5,1},{9,13},{13,9},{2,6},{6,2},{1... | collective-permute-start | bytes 1572872 | tf_op jit(solution)/shard_map/ppermute | solution.py:293
  550.1 68.1 %collective-permute-start.8 = (bf16[512,2304]{1,0:T(8,128)(2,1)S(1)}, bf16[512,2304]{1,0:T(8,128)(2,1)S(1)}, u32[]{:S(2)}, u32[]{:S(2)}) collective-permute-start(bf16[512,2304]{1,0:T(8,128)(2,1)S(1)} %fusion.9.h_ref), channel_id=1, source_target_pairs={{0,4},{4,0},{8,12},{12,8},{1,5},{5,1},{9,13},{13,9},{2,6},{6,2},{1... | collective-permute-start | bytes 7077896 | tf_op jit(solution)/shard_map/ppermute | solution.py:328
  686.5 82.5 %collective-permute-start.9 = (f32[256,2304]{1,0:T(8,128)}, f32[256,2304]{1,0:T(8,128)S(1)}, u32[]{:S(2)}, u32[]{:S(2)}) collective-permute-start(f32[256,2304]{1,0:T(8,128)} %ff_part.18), channel_id=1, source_target_pairs={{0,4},{4,0},{8,12},{12,8},{1,5},{5,1},{9,13},{13,9},{2,6},{6,2},{1... | collective-permute-start | bytes 7077896 | tf_op jit(solution)/shard_map/ppermute | solution.py:338
  702.1 87.6 %collective-permute-start.10 = (f32[256,2304]{1,0:T(8,128)}, f32[256,2304]{1,0:T(8,128)S(1)}, u32[]{:S(2)}, u32[]{:S(2)}) collective-permute-start(f32[256,2304]{1,0:T(8,128)} %ff_part.19), channel_id=1, source_target_pairs={{0,4},{4,0},{8,12},{12,8},{1,5},{5,1},{9,13},{13,9},{2,6},{6,2},{1... | collective-permute-start | bytes 7077896 | tf_op jit(solution)/shard_map/ppermute | solution.py:338
  847.7 54.2 %collective-permute-start.14 = (bf16[256,2304]{1,0:T(8,128)(2,1)}, bf16[256,2304]{1,0:T(8,128)(2,1)S(1)}, u32[]{:S(2)}, u32[]{:S(2)}) collective-permute-start(bf16[256,2304]{1,0:T(8,128)(2,1)} %collective-permute-done.12), channel_id=1, source_target_pairs={{0,12},{4,0},{8,4},{12,8},{1,13},{5,1},{9,5},{13,9},{2,14},{6,2},{... | collective-permute-start | bytes 3538952 | tf_op jit(solution)/shard_map/ppermute | solution.py:364
  959.6 54.5 %collective-permute-start.18 = (bf16[512,512]{1,0:T(8,128)(2,1)S(1)}, bf16[512,512]{1,0:T(8,128)(2,1)S(1)}, u32[]{:S(2)}, u32[]{:S(2)}) collective-permute-start(bf16[512,512]{1,0:T(8,128)(2,1)S(1)} %maximum_maximum_fusion.1), channel_id=1, source_target_pairs={{0,1},{1,0},{2,3},{3,2},{4,5},{5,4},{6,7},{7,6},{8,9},{9,8},{10,11... | collective-permute-start | bytes 1572872 | tf_op jit(solution)/shard_map/ppermute | solution.py:355
  960.2 54.0 %collective-permute-start.17 = (bf16[1536,512]{1,0:T(8,128)(2,1)S(1)}, bf16[1536,512]{1,0:T(8,128)(2,1)S(1)}, u32[]{:S(2)}, u32[]{:S(2)}) collective-permute-start(bf16[1536,512]{1,0:T(8,128)(2,1)S(1)} %maximum_dynamic-update-slice_fusion), channel_id=1, source_target_pairs={{0,1},{1,0},{2,3},{3,2},{4,5},{5,4},{6,7},{7,6},{8,9},{9,8},{10,11... | collective-permute-start | bytes 4718600 | tf_op jit(solution)/shard_map/ppermute | solution.py:355
  1220.3 72.6 %collective-permute-start.29 = (f32[256,2304]{1,0:T(8,128)}, f32[256,2304]{1,0:T(8,128)S(1)}, u32[]{:S(2)}, u32[]{:S(2)}) collective-permute-start(f32[256,2304]{1,0:T(8,128)} %ff_part.23), channel_id=1, source_target_pairs={{0,4},{4,0},{8,12},{12,8},{1,5},{5,1},{9,13},{13,9},{2,6},{6,2},{1... | collective-permute-start | bytes 7077896 | tf_op jit(solution)/shard_map/ppermute | solution.py:386
  1239.8 83.2 %collective-permute-start.31 = (f32[256,2304]{1,0:T(8,128)}, f32[256,2304]{1,0:T(8,128)S(1)}, u32[]{:S(2)}, u32[]{:S(2)}) collective-permute-start(f32[256,2304]{1,0:T(8,128)} %ff_part.25), channel_id=1, source_target_pairs={{0,4},{4,0},{8,12},{12,8},{1,5},{5,1},{9,13},{13,9},{2,6},{6,2},{1... | collective-permute-start | bytes 7077896 | tf_op jit(solution)/shard_map/ppermute | solution.py:389
  (55 other events, 1180.5 us)
Sparse Core Ops, SparseCore 0:
  13.1 173.4 all-gather.22
  188.5 38.7 all-gather.16
  229.2 63.6 all-gather.14
  294.7 41.2 all-gather.12
  337.7 67.3 all-gather.10
  407.8 163.9 all-gather.24
  573.7 62.5 all-gather.20
  638.2 108.5 all-gather.18

commit v2 on v1

--- a/solution.py
+++ b/solution.py
@@ -346,12 +346,12 @@
         sin_half = sine.reshape(2 * num_tp, half, HALF)
         qkv1 = jnp.zeros((2 * num_tp, half, heads_w + 2 * HEAD), BF16)
 
-        def project(rows, block):
+        def project(rows, weight, block):
             pick = functools.partial(lax.dynamic_index_in_dim, index=block, axis=0, keepdims=False)
-            return rotate(dot32(rows, weight).astype(BF16), pick(cos_half), pick(sin_half), 3)
-
-        def exchange(pieces):
-            kv = jnp.concatenate([p[:, heads_w:] for p in pieces], axis=0)
+            out = dot32(rows, weight).astype(BF16)
+            return rotate(out, pick(cos_half), pick(sin_half), 3)
+
+        def exchange(kv):
             core = lax.ppermute(kv, 'sp', sp_core)
             far = lax.ppermute(kv, 'sp', sp_far)
             return core, far
@@ -363,12 +363,14 @@
                 up = lax.ppermute(up, 'tp', ring_up)
                 dn = lax.ppermute(dn, 'tp', ring_dn)
             for rows, block in ((up, 2 * lax.rem(z - s + num_tp, num_tp)), (dn, 2 * lax.rem(z + s, num_tp) + 1)):
-                out = project(rows, block)
+                out = project(rows, weight, block)
                 done.append(out)
                 qkv1 = place(qkv1, out, block)
             if s == 2:
-                core_a, far_a = exchange(done)
-        core_b, far_b = exchange(done[6:])
+                kv_a = jnp.concatenate([p[:, heads_w:] for p in done], axis=0)
+                kv_a, weight = lax.optimization_barrier((kv_a, weight))
+                core_a, far_a = exchange(kv_a)
+        core_b, far_b = exchange(jnp.concatenate([p[:, heads_w:] for p in done[6:]], axis=0))
         diag_a = lax.ppermute(far_a, 'sp', sp_core)
         diag_b = lax.ppermute(far_b, 'sp', sp_core)
         qkv1 = qkv1.reshape(num, heads_w + 2 * HEAD)

time: 1500 us -> 1490 us (level)
  the two profiles are of different devices: /device:TPU:7 before, /device:TPU:5 now
where the time goes in v2:
time: 1490 us; the launch traced here: 1480 us
  waiting for transfers between devices  811 us (54%)
  Pallas kernels  337 us (23%)
  starting transfers between devices  129 us (9%)
  local copies, waits for them, and re-layouts  79.7 us (5%)
  other arithmetic  54.2 us (4%)
  matrix products  52.2 us (4%)
  between operations  15.3 us (1%)
    ppermute x6, waiting for transfers between devices, cross(): return lax.ppermute(piece, 'tp', flip[2])  350 us
    pallas_call x13, Pallas kernels, ff_part(): pl.pallas_call(functools.partial(ff_kernel, init is not None), out_shape=...  263 us
    ppermute x6, waiting for transfers between devices, layers(): dn = lax.ppermute(dn, 'tp', ring_dn)  159 us
    ppermute x6, waiting for transfers between devices, layers(): up = lax.ppermute(up, 'tp', ring_up)  117 us
    ppermute x1, starting transfers between devices, layers(): theirs = lax.ppermute(h2, 'tp', flip[1])  94.2 us
    pallas_call x1, Pallas kernels, causal_attention(): pl.pallas_call(causal_kernel, out_shape=jax.ShapeDtypeStruct((num, 2 * HE...  60.8 us
    dot_general x11, matrix products, dot32(): return jnp.dot(a, b, preferred_element_type=F32)  52.2 us
    ppermute x1, waiting for transfers between devices, layers(): theirs = lax.ppermute(h2, 'tp', flip[1])  50.3 us
  transfers between devices with their start and end apart: 46, of which 27 were waited for; matrix products, arithmetic and copies ran while one was open for 11% of the time, Pallas kernels for 22%

profile of v2, /device:TPU:5, one launch (start us, length us, event | category | flops | bytes accessed | tf_op | source)
XLA Modules:
  0.0 1478.2 jit_solution(11472382010723985379)
XLA Ops:
  17.6 35.0 %collective-permute-done.7 = bf16[144,2304]{1,0:T(8,128)(2,1)S(1)} collective-permute-done((bf16[144,2304]{1,0:T(8,128)(2,1)S(1)}, bf16[144,2304]{1,0:T(8,128)(2,1)S(1)}, u32[]{:S(2)}, u32[]{:S(2)}) %collective-permute-start.7) | collective-permute-done | bytes 663584 | tf_op jit(solution)/shard_map/ppermute | solution.py:276
  56.5 71.3 %collective-permute-done.6 = bf16[288,2304]{1,0:T(8,128)(2,1)} collective-permute-done((bf16[288,2304]{1,0:T(8,128)(2,1)S(1)}, bf16[288,2304]{1,0:T(8,128)(2,1)}, u32[]{:S(2)}, u32[]{:S(2)}) %collective-permute-start.6) | collective-permute-done | bytes 1327136 | tf_op jit(solution)/shard_map/ppermute | solution.py:276
  127.9 57.2 %collective-permute-done.5 = bf16[144,2304]{1,0:T(8,128)(2,1)} collective-permute-done((bf16[144,2304]{1,0:T(8,128)(2,1)}, bf16[144,2304]{1,0:T(8,128)(2,1)}, u32[]{:S(2)}, u32[]{:S(2)}) %collective-permute-start.5) | collective-permute-done | bytes 663584 | tf_op jit(solution)/shard_map/ppermute | solution.py:276
  186.4 59.6 %collective-permute-done.4 = bf16[288,2304]{1,0:T(8,128)(2,1)} collective-permute-done((bf16[288,2304]{1,0:T(8,128)(2,1)S(1)}, bf16[288,2304]{1,0:T(8,128)(2,1)}, u32[]{:S(2)}, u32[]{:S(2)}) %collective-permute-start.4) | collective-permute-done | bytes 1327136 | tf_op jit(solution)/shard_map/ppermute | solution.py:276
  248.4 59.8 %collective-permute-done.27 = bf16[288,2304]{1,0:T(8,128)(2,1)S(1)} collective-permute-done((bf16[288,2304]{1,0:T(8,128)(2,1)S(1)}, bf16[288,2304]{1,0:T(8,128)(2,1)S(1)}, u32[]{:S(2)}, u32[]{:S(2)}) %collective-permute-start.27) | collective-permute-done | bytes 1327136 | tf_op jit(solution)/shard_map/ppermute | solution.py:276
  420.3 94.2 %collective-permute-start.8 = (bf16[512,2304]{1,0:T(8,128)(2,1)S(1)}, bf16[512,2304]{1,0:T(8,128)(2,1)}, u32[]{:S(2)}, u32[]{:S(2)}) collective-permute-start(bf16[512,2304]{1,0:T(8,128)(2,1)S(1)} %fusion.9.h_ref), channel_id=1, source_target_pairs={{0,4},{4,0},{8,12},{12,8},{1,5},{5,1},{9,13},{13,9},{2,6},{6,2},{1... | collective-permute-start | bytes 7077896 | tf_op jit(solution)/shard_map/ppermute | solution.py:328
  514.5 67.0 %collective-permute-done.26 = bf16[288,4608]{1,0:T(8,128)(2,1)} collective-permute-done((bf16[288,4608]{1,0:T(8,128)(2,1)}, bf16[288,4608]{1,0:T(8,128)(2,1)}, u32[]{:S(2)}, u32[]{:S(2)}) %collective-permute-start.26) | collective-permute-done | bytes 2654240 | tf_op jit(solution)/shard_map/ppermute | solution.py:276
  585.1 50.3 %collective-permute-done.8.h_ref = bf16[512,2304]{1,0:T(8,128)(2,1)} collective-permute-done((bf16[512,2304]{1,0:T(8,128)(2,1)S(1)}, bf16[512,2304]{1,0:T(8,128)(2,1)}, u32[]{:S(2)}, u32[]{:S(2)}) %collective-permute-start.8) | collective-permute-done | bytes 2359328 | tf_op jit(solution)/shard_map/ppermute | solution.py:328
  635.5 25.9 %ff_part.16.rest_0_ = f32[512,2304]{1,0:T(8,128)} custom-call(bf16[512,2304]{1,0:T(8,128)(2,1)} %collective-permute-done.8.h_ref, bf16[2,2304,2304]{2,1,0:T(8,128)(2,1)} %g_ref.9, bf16[2,2304,2304]{2,1,0:T(8,128)(2,1)} %u_ref.9, bf16[2,2304,2304]{2,1,0:T(8,128)(2,1)} %d_ref.9), custom_call_target="tpu_custom_call" | custom-call | flops 16307453952 | bytes 31850496 | tf_op jit(solution)/shard_map/ff_part/pallas_call | solution.py:210
  714.4 26.1 %ff_part.13.rest_0_ = f32[512,2304]{1,0:T(8,128)} custom-call(bf16[512,2304]{1,0:T(8,128)(2,1)} %copy-done, bf16[2,2304,2304]{2,1,0:T(8,128)(2,1)} %g_ref.9, bf16[2,2304,2304]{2,1,0:T(8,128)(2,1)} %u_ref.9, bf16[2,2304,2304]{2,1,0:T(8,128)(2,1)} %d_ref.9), custom_call_target="tpu_custom_call" | custom-call | flops 16307453952 | bytes 31850496 | tf_op jit(solution)/shard_map/ff_part/pallas_call | solution.py:210
  836.6 30.6 %collective-permute-done.12 = bf16[256,2304]{1,0:T(8,128)(2,1)} collective-permute-done((bf16[256,2304]{1,0:T(8,128)(2,1)}, bf16[256,2304]{1,0:T(8,128)(2,1)}, u32[]{:S(2)}, u32[]{:S(2)}) %collective-permute-start.12) | collective-permute-done | bytes 1179680 | tf_op jit(solution)/shard_map/ppermute | solution.py:364
  889.4 25.0 %collective-permute-done.14 = bf16[256,2304]{1,0:T(8,128)(2,1)S(1)} collective-permute-done((bf16[256,2304]{1,0:T(8,128)(2,1)}, bf16[256,2304]{1,0:T(8,128)(2,1)S(1)}, u32[]{:S(2)}, u32[]{:S(2)}) %collective-permute-start.14) | collective-permute-done | bytes 1179680 | tf_op jit(solution)/shard_map/ppermute | solution.py:364
  923.2 25.2 %collective-permute-done.16 = bf16[256,2304]{1,0:T(8,128)(2,1)S(1)} collective-permute-done((bf16[256,2304]{1,0:T(8,128)(2,1)S(1)}, bf16[256,2304]{1,0:T(8,128)(2,1)S(1)}, u32[]{:S(2)}, u32[]{:S(2)}) %collective-permute-start.16) | collective-permute-done | bytes 1179680 | tf_op jit(solution)/shard_map/ppermute | solution.py:364
  949.9 23.8 %collective-permute-done.15 = bf16[256,2304]{1,0:T(8,128)(2,1)S(1)} collective-permute-done((bf16[256,2304]{1,0:T(8,128)(2,1)S(1)}, bf16[256,2304]{1,0:T(8,128)(2,1)S(1)}, u32[]{:S(2)}, u32[]{:S(2)}) %collective-permute-start.15) | collective-permute-done | bytes 1179680 | tf_op jit(solution)/shard_map/ppermute | solution.py:363
  1003.5 60.8 %causal_attn.1 = bf16[2048,512]{1,0:T(8,128)(2,1)} custom-call(s32[1]{0:T(128)} %bitcast.3.c_ref, bf16[2048,512]{1,0:T(8,128)(2,1)} %get-tuple-element.70.q_ref, bf16[2048,512]{1,0:T(8,128)(2,1)} %get-tuple-element.69.kl_ref, bf16[1536,512]{1,0:T(8,128)(2,1)} %copy-done.26, bf16[512,512]{1,0:T(8,128)(2,1)} %copy-done.29, bf16[1536,512]{1,0:T(8,128)(2,1)} %copy-done.25, ...), custom_call_target="tpu_custom_call" | custom-call | flops 34359738368 | bytes 10485760 | tf_op jit(solution)/shard_map/causal_attn/pallas_call | solution.py:153
  1068.5 23.0 %collective-permute-done.23 = bf16[512,512]{1,0:T(8,128)(2,1)S(1)} collective-permute-done((bf16[512,512]{1,0:T(8,128)(2,1)S(1)}, bf16[512,512]{1,0:T(8,128)(2,1)S(1)}, u32[]{:S(2)}, u32[]{:S(2)}) %collective-permute-start.23) | collective-permute-done | bytes 524320 | tf_op jit(solution)/shard_map/ppermute | solution.py:293
  1227.5 25.7 %ff_part.20.rest_0_ = f32[512,2304]{1,0:T(8,128)} custom-call(bf16[512,2304]{1,0:T(8,128)(2,1)} %copy-done.1, bf16[2,2304,2304]{2,1,0:T(8,128)(2,1)} %g_ref.9, bf16[2,2304,2304]{2,1,0:T(8,128)(2,1)} %u_ref.9, bf16[2,2304,2304]{2,1,0:T(8,128)(2,1)} %d_ref.9), custom_call_target="tpu_custom_call" | custom-call | flops 16307453952 | bytes 31850496 | tf_op jit(solution)/shard_map/ff_part/pallas_call | solution.py:210
  1253.2 27.3 %ff_part.21 = f32[512,2304]{1,0:T(8,128)} custom-call(bf16[512,2304]{1,0:T(8,128)(2,1)} %copy-done.1, bf16[2304,4608]{1,0:T(8,128)(2,1)} %all-gather.19.cloned.1.call-done.g_ref.u_ref, bf16[2304,4608]{1,0:T(8,128)(2,1)} %all-gather.19.cloned.1.call-done.g_ref.u_ref, bf16[2304,2304]{1,0:T(8,128)(2,1)} %all-gather.21.cloned.1.call-done.d_ref, ...), custom_call_target="tpu_custom_call" | custom-call | flops 16307453952 | bytes 31850496 | tf_op jit(solution)/shard_map/ff_part/pallas_call | solution.py:210
  1280.5 30.1 %collective-permute-done.31 = f32[256,2304]{1,0:T(8,128)S(1)} collective-permute-done((f32[256,2304]{1,0:T(8,128)}, f32[256,2304]{1,0:T(8,128)S(1)}, u32[]{:S(2)}, u32[]{:S(2)}) %collective-permute-start.31) | collective-permute-done | bytes 2359328 | tf_op jit(solution)/shard_map/ppermute | solution.py:391
  1319.3 22.4 %collective-permute-done.32 = bf16[256,2304]{1,0:T(8,128)(2,1)S(1)} collective-permute-done((bf16[256,2304]{1,0:T(8,128)(2,1)S(1)}, bf16[256,2304]{1,0:T(8,128)(2,1)S(1)}, u32[]{:S(2)}, u32[]{:S(2)}) %collective-permute-start.32) | collective-permute-done | bytes 1179680 | tf_op jit(solution)/shard_map/ppermute | solution.py:399
  1341.7 25.4 %collective-permute-done.33 = bf16[256,2304]{1,0:T(8,128)(2,1)S(1)} collective-permute-done((bf16[256,2304]{1,0:T(8,128)(2,1)S(1)}, bf16[256,2304]{1,0:T(8,128)(2,1)S(1)}, u32[]{:S(2)}, u32[]{:S(2)}) %collective-permute-start.33) | collective-permute-done | bytes 1179680 | tf_op jit(solution)/shard_map/ppermute | solution.py:400
  1369.8 22.6 %collective-permute-done.34 = bf16[256,2304]{1,0:T(8,128)(2,1)S(1)} collective-permute-done((bf16[256,2304]{1,0:T(8,128)(2,1)S(1)}, bf16[256,2304]{1,0:T(8,128)(2,1)S(1)}, u32[]{:S(2)}, u32[]{:S(2)}) %collective-permute-start.34) | collective-permute-done | bytes 1179680 | tf_op jit(solution)/shard_map/ppermute | solution.py:399
  1392.3 26.6 %collective-permute-done.35 = bf16[256,2304]{1,0:T(8,128)(2,1)S(1)} collective-permute-done((bf16[256,2304]{1,0:T(8,128)(2,1)S(1)}, bf16[256,2304]{1,0:T(8,128)(2,1)S(1)}, u32[]{:S(2)}, u32[]{:S(2)}) %collective-permute-start.35) | collective-permute-done | bytes 1179680 | tf_op jit(solution)/shard_map/ppermute | solution.py:400
  1444.0 26.0 %collective-permute-done.37 = bf16[256,2304]{1,0:T(8,128)(2,1)S(1)} collective-permute-done((bf16[256,2304]{1,0:T(8,128)(2,1)S(1)}, bf16[256,2304]{1,0:T(8,128)(2,1)S(1)}, u32[]{:S(2)}, u32[]{:S(2)}) %collective-permute-start.37) | collective-permute-done | bytes 1179680 | tf_op jit(solution)/shard_map/ppermute | solution.py:400
  (276 shorter events, 521.9 us)
Async XLA Ops:
  7.2 401.9 %all-gather.23.cloned.1.call-start = ((), (), s32[]{:S(2)}) async-start(), calls=%async_computation.6 | async-start | bytes 9732096 | tf_op jit(solution)/shard_map/all_gather | solution.py:255
  13.0 648.3 %all-gather.17.cloned.1.call-start = ((), (), s32[]{:S(2)}) async-start(), calls=%async_computation.3 | async-start | bytes 5971968 | tf_op jit(solution)/shard_map/all_gather | solution.py:258
  53.5 607.9 %all-gather.15.cloned.1.call-start = ((), (), s32[]{:S(2)}) async-start(), calls=%async_computation.2 | async-start | bytes 11943936 | tf_op jit(solution)/shard_map/all_gather | solution.py:258
  56.4 71.3 %collective-permute-start.6 = (bf16[288,2304]{1,0:T(8,128)(2,1)S(1)}, bf16[288,2304]{1,0:T(8,128)(2,1)}, u32[]{:S(2)}, u32[]{:S(2)}) collective-permute-start(bf16[288,2304]{1,0:T(8,128)(2,1)S(1)} %pad_maximum_fusion.5), channel_id=1, source_target_pairs={{0,8},{4,12},{8,0},{12,4},{1,9},{5,13},{9,1},{13,5},{2,10},{6,14},... | collective-permute-start | bytes 3981320 | tf_op jit(solution)/shard_map/ppermute | solution.py:276
  127.7 559.5 %all-gather.13.cloned.1.call-start = ((), (), s32[]{:S(2)}) async-start(), calls=%async_computation.1 | async-start | bytes 5971968 | tf_op jit(solution)/shard_map/all_gather | solution.py:258
  127.8 57.3 %collective-permute-start.5 = (bf16[144,2304]{1,0:T(8,128)(2,1)}, bf16[144,2304]{1,0:T(8,128)(2,1)}, u32[]{:S(2)}, u32[]{:S(2)}) collective-permute-start(bf16[144,2304]{1,0:T(8,128)(2,1)} %get-tuple-element.49), channel_id=1, source_target_pairs={{0,8},{4,12},{8,0},{12,4},{1,9},{5,13},{9,1},{13,5},{2,10},{6,14},... | collective-permute-start | bytes 1990664 | tf_op jit(solution)/shard_map/ppermute | solution.py:276
  185.1 502.2 %all-gather.11.cloned.1.call-start = ((), (), s32[]{:S(2)}) async-start(), calls=%async_computation | async-start | bytes 11943936 | tf_op jit(solution)/shard_map/all_gather | solution.py:258
  186.3 59.6 %collective-permute-start.4 = (bf16[288,2304]{1,0:T(8,128)(2,1)S(1)}, bf16[288,2304]{1,0:T(8,128)(2,1)}, u32[]{:S(2)}, u32[]{:S(2)}) collective-permute-start(bf16[288,2304]{1,0:T(8,128)(2,1)S(1)} %pad_maximum_fusion.4), channel_id=1, source_target_pairs={{0,8},{4,12},{8,0},{12,4},{1,9},{5,13},{9,1},{13,5},{2,10},{6,14},... | collective-permute-start | bytes 3981320 | tf_op jit(solution)/shard_map/ppermute | solution.py:276
  246.0 851.5 %all-gather.25.cloned.1.call-start = ((), (), s32[]{:S(2)}) async-start(), calls=%async_computation.7 | async-start | bytes 9732096 | tf_op jit(solution)/shard_map/all_gather | solution.py:255
  246.8 942.2 %all-gather.21.cloned.1.call-start = ((), (), s32[]{:S(2)}) async-start(), calls=%async_computation.5 | async-start | bytes 11943936 | tf_op jit(solution)/shard_map/all_gather | solution.py:258
  248.3 59.9 %collective-permute-start.27 = (bf16[288,2304]{1,0:T(8,128)(2,1)S(1)}, bf16[288,2304]{1,0:T(8,128)(2,1)S(1)}, u32[]{:S(2)}, u32[]{:S(2)}) collective-permute-start(bf16[288,2304]{1,0:T(8,128)(2,1)S(1)} %dynamic-slice_bitcast_fusion), channel_id=1, source_target_pairs={{0,8},{4,12},{8,0},{12,4},{1,9},{5,13},{9,1},{13,5},{2,10},{6,14},... | collective-permute-start | bytes 3981320 | tf_op jit(solution)/shard_map/ppermute | solution.py:276
  309.3 879.7 %all-gather.19.cloned.1.call-start = ((), (), s32[]{:S(2)}) async-start(), calls=%async_computation.4 | async-start | bytes 23887872 | tf_op jit(solution)/shard_map/all_gather | solution.py:258
  386.1 195.5 %collective-permute-start.26 = (bf16[288,4608]{1,0:T(8,128)(2,1)}, bf16[288,4608]{1,0:T(8,128)(2,1)}, u32[]{:S(2)}, u32[]{:S(2)}) collective-permute-start(bf16[288,4608]{1,0:T(8,128)(2,1)} %pad_maximum_fusion.1), channel_id=1, source_target_pairs={{0,8},{4,12},{8,0},{12,4},{1,9},{5,13},{9,1},{13,5},{2,10},{6,14},... | collective-permute-start | bytes 7962632 | tf_op jit(solution)/shard_map/ppermute | solution.py:276
  420.3 215.2 %collective-permute-start.8 = (bf16[512,2304]{1,0:T(8,128)(2,1)S(1)}, bf16[512,2304]{1,0:T(8,128)(2,1)}, u32[]{:S(2)}, u32[]{:S(2)}) collective-permute-start(bf16[512,2304]{1,0:T(8,128)(2,1)S(1)} %fusion.9.h_ref), channel_id=1, source_target_pairs={{0,4},{4,0},{8,12},{12,8},{1,5},{5,1},{9,13},{13,9},{2,6},{6,2},{1... | collective-permute-start | bytes 7077896 | tf_op jit(solution)/shard_map/ppermute | solution.py:328
  700.0 80.4 %collective-permute-start.9 = (f32[256,2304]{1,0:T(8,128)}, f32[256,2304]{1,0:T(8,128)S(1)}, u32[]{:S(2)}, u32[]{:S(2)}) collective-permute-start(f32[256,2304]{1,0:T(8,128)} %ff_part.18), channel_id=1, source_target_pairs={{0,4},{4,0},{8,12},{12,8},{1,5},{5,1},{9,13},{13,9},{2,6},{6,2},{1... | collective-permute-start | bytes 7077896 | tf_op jit(solution)/shard_map/ppermute | solution.py:338
  713.0 88.4 %collective-permute-start.10 = (f32[256,2304]{1,0:T(8,128)}, f32[256,2304]{1,0:T(8,128)S(1)}, u32[]{:S(2)}, u32[]{:S(2)}) collective-permute-start(f32[256,2304]{1,0:T(8,128)} %ff_part.19), channel_id=1, source_target_pairs={{0,4},{4,0},{8,12},{12,8},{1,5},{5,1},{9,13},{13,9},{2,6},{6,2},{1... | collective-permute-start | bytes 7077896 | tf_op jit(solution)/shard_map/ppermute | solution.py:338
  812.7 54.5 %collective-permute-start.12 = (bf16[256,2304]{1,0:T(8,128)(2,1)}, bf16[256,2304]{1,0:T(8,128)(2,1)}, u32[]{:S(2)}, u32[]{:S(2)}) collective-permute-start(bf16[256,2304]{1,0:T(8,128)(2,1)} %get-tuple-element.75), channel_id=1, source_target_pairs={{0,12},{4,0},{8,4},{12,8},{1,13},{5,1},{9,5},{13,9},{2,14},{6,2},{... | collective-permute-start | bytes 3538952 | tf_op jit(solution)/shard_map/ppermute | solution.py:364
  918.9 56.9 %collective-permute-start.19 = (bf16[1536,512]{1,0:T(8,128)(2,1)S(1)}, bf16[1536,512]{1,0:T(8,128)(2,1)S(1)}, u32[]{:S(2)}, u32[]{:S(2)}) collective-permute-start(bf16[1536,512]{1,0:T(8,128)(2,1)S(1)} %maximum_dynamic-update-slice_fusion), channel_id=1, source_target_pairs={{0,2},{1,3},{4,6},{5,7},{8,10},{9,11},{12,14},{13,15},{16,18},{17,... | collective-permute-start | bytes 4718600 | tf_op jit(solution)/shard_map/ppermute | solution.py:356
  920.4 81.0 %collective-permute-start.17 = (bf16[1536,512]{1,0:T(8,128)(2,1)S(1)}, bf16[1536,512]{1,0:T(8,128)(2,1)S(1)}, u32[]{:S(2)}, u32[]{:S(2)}) collective-permute-start(bf16[1536,512]{1,0:T(8,128)(2,1)S(1)} %maximum_dynamic-update-slice_fusion), channel_id=1, source_target_pairs={{0,1},{1,0},{2,3},{3,2},{4,5},{5,4},{6,7},{7,6},{8,9},{9,8},{10,11... | collective-permute-start | bytes 4718600 | tf_op jit(solution)/shard_map/ppermute | solution.py:355
  921.3 52.5 %collective-permute-start.15 = (bf16[256,2304]{1,0:T(8,128)(2,1)S(1)}, bf16[256,2304]{1,0:T(8,128)(2,1)S(1)}, u32[]{:S(2)}, u32[]{:S(2)}) collective-permute-start(bf16[256,2304]{1,0:T(8,128)(2,1)S(1)} %collective-permute-done.13), channel_id=1, source_target_pairs={{0,4},{4,8},{8,12},{12,0},{1,5},{5,9},{9,13},{13,1},{2,6},{6,10},{... | collective-permute-start | bytes 3538952 | tf_op jit(solution)/shard_map/ppermute | solution.py:363
  1207.7 72.8 %collective-permute-start.29 = (f32[256,2304]{1,0:T(8,128)}, f32[256,2304]{1,0:T(8,128)S(1)}, u32[]{:S(2)}, u32[]{:S(2)}) collective-permute-start(f32[256,2304]{1,0:T(8,128)} %ff_part.23), channel_id=1, source_target_pairs={{0,4},{4,0},{8,12},{12,8},{1,5},{5,1},{9,13},{13,9},{2,6},{6,2},{1... | collective-permute-start | bytes 7077896 | tf_op jit(solution)/shard_map/ppermute | solution.py:388
  1227.2 83.4 %collective-permute-start.31 = (f32[256,2304]{1,0:T(8,128)}, f32[256,2304]{1,0:T(8,128)S(1)}, u32[]{:S(2)}, u32[]{:S(2)}) collective-permute-start(f32[256,2304]{1,0:T(8,128)} %ff_part.25), channel_id=1, source_target_pairs={{0,4},{4,0},{8,12},{12,8},{1,5},{5,1},{9,13},{13,9},{2,6},{6,2},{1... | collective-permute-start | bytes 7077896 | tf_op jit(solution)/shard_map/ppermute | solution.py:391
  1314.8 52.3 %collective-permute-start.33 = (bf16[256,2304]{1,0:T(8,128)(2,1)S(1)}, bf16[256,2304]{1,0:T(8,128)(2,1)S(1)}, u32[]{:S(2)}, u32[]{:S(2)}) collective-permute-start(bf16[256,2304]{1,0:T(8,128)(2,1)S(1)} %get-tuple-element.71), channel_id=1, source_target_pairs={{0,12},{4,0},{8,4},{12,8},{1,13},{5,1},{9,5},{13,9},{2,14},{6,2},{... | collective-permute-start | bytes 3538952 | tf_op jit(solution)/shard_map/ppermute | solution.py:400
  1367.1 51.9 %collective-permute-start.35 = (bf16[256,2304]{1,0:T(8,128)(2,1)S(1)}, bf16[256,2304]{1,0:T(8,128)(2,1)S(1)}, u32[]{:S(2)}, u32[]{:S(2)}) collective-permute-start(bf16[256,2304]{1,0:T(8,128)(2,1)S(1)} %collective-permute-done.33), channel_id=1, source_target_pairs={{0,12},{4,0},{8,4},{12,8},{1,13},{5,1},{9,5},{13,9},{2,14},{6,2},{... | collective-permute-start | bytes 3538952 | tf_op jit(solution)/shard_map/ppermute | solution.py:400
  (55 other events, 1104.6 us)
Sparse Core Ops, SparseCore 0:
  13.1 173.4 all-gather.22
  188.6 39.4 all-gather.16
  230.0 63.4 all-gather.14
  295.2 41.4 all-gather.12
  338.4 66.4 all-gather.10
  407.7 189.1 all-gather.24
  598.8 62.1 all-gather.20
  662.9 108.0 all-gather.18
